TPU v7x, 128 devices: a whole 4x4x4 slice. The times are simulated.
128 devices in a mesh: fsdp: 32 (over x, y, core), dp: 4 (over z).
Axes of the slice: x: 4, y: 4, z: 4, core: 2. Of those that a mesh axis runs over, the one named last changes fastest.
Arguments:
- tokens: bfloat16 [65536, 4096], P(('fsdp', 'dp')), may hold values from -40 to 40
- cotangent: bfloat16 [65536, 2048], P(('fsdp', 'dp')), may hold values from -20 to 20
- weight: bfloat16 [4096, 2048], P('fsdp'), may hold values from -1 to 1
- left_vector: float32 [4096], P('fsdp'), may hold values from -6 to 6
Outputs:
- layer_out: bfloat16 [65536, 2048], P(('fsdp', 'dp'))
- input_grad: bfloat16 [65536, 4096], P(('fsdp', 'dp'))
- update: bfloat16 [4096, 2048], P('fsdp')
- left_next: float32 [4096], P('fsdp')
- right_next: float32 [2048], replicated
All inputs are finite; a program needn't handle non-finite values.
Results may differ from a plain program's by a relative error of at most 0.015.
Values may be sent and summed in bfloat16 or wider, within the bound.
A program may use at most 128 MiB of HBM per device.

v0:
```python
import jax
import jax.numpy as jnp
from jax import lax
from jax.sharding import Mesh
from jax.sharding import PartitionSpec as P

FSDP = ("fsdp_0", "fsdp_1", "fsdp_2")
FSDP_DP = ("fsdp_0", "fsdp_1", "fsdp_2", "dp")
epsilon = 1e-06


def sent_to_all(value, axis):
    copies = jnp.broadcast_to(value, (lax.axis_size(axis), *value.shape))
    return lax.all_to_all(copies, axis, split_axis=0, concat_axis=0, tiled=True)


def taken_together(value, axis):
    return sent_to_all(value, axis).sum(axis=0)


def in_order(blocks, dim):
    blocks = jnp.moveaxis(blocks, 0, dim)
    dims = blocks.shape
    return blocks.reshape(*dims[:dim], dims[dim] * dims[dim + 1], *dims[dim + 2 :])


def gather_in_order(value, axes, order):
    blocks = value[None]
    for k in order:
        blocks = lax.all_gather(blocks, axes[k], axis=0, tiled=True)
    block = [lax.axis_size(axes[k]) for k in reversed(order)]
    blocks = blocks.reshape(*block, *value.shape)
    turned = sorted(range(len(order)), key=lambda place: order[len(order) - 1 - place])
    return blocks.transpose(*turned, *range(len(order), blocks.ndim)).reshape(-1, *value.shape)


def whole_of(value, axes, order, dim):
    return in_order(gather_in_order(value, axes, order), dim)


def over_copies(value, axis):
    everything = sent_to_all(value, axis)
    return jnp.sum(everything.astype(jnp.float32), axis=0)


def packed_total(arrays, axis):
    flat, at, done = (jnp.concatenate([a.reshape(-1) for a in arrays]), 0, [])
    running = taken_together(flat, axis)
    for a in arrays:
        done.append(running[at : at + a.size].reshape(a.shape))
        at += a.size
    return tuple(done)


def per_device(tokens, cotangent, weight, left_vector):
    weight_wide = weight.astype(jnp.float32)
    part_right = jnp.dot(left_vector, weight_wide)
    right_raw = taken_together(part_right, FSDP)
    right_next = right_raw / jnp.sqrt(jnp.sum(right_raw * right_raw) + epsilon)
    left_raw = jnp.dot(weight_wide, right_next)
    left_sq = taken_together(jnp.sum(left_raw * left_raw), FSDP)
    spectral = jnp.sqrt(left_sq + epsilon)
    left_next = left_raw / spectral
    gathered = whole_of(weight, (("fsdp_0", "fsdp_1"), "fsdp_2"), (0, 1), 0)
    product = jnp.dot(tokens, gathered, preferred_element_type=jnp.float32)
    layer_out = (product / spectral).astype(jnp.bfloat16)
    back_prod = lax.dot_general(
        cotangent, gathered, (((1,), (1,)), ((), ())), preferred_element_type=jnp.float32
    )
    input_grad = (back_prod / spectral).astype(jnp.bfloat16)
    shard_rows = weight.shape[0]
    shard_sum = lax.psum_scatter(
        lax.dot_general(
            tokens, cotangent, (((0,), (0,)), ((), ())), preferred_element_type=jnp.float32
        ).astype(jnp.bfloat16),
        FSDP,
        scatter_dimension=0,
        tiled=True,
    )
    grad_sum = over_copies(shard_sum, "dp").astype(jnp.float32)
    entry_count = shard_rows * lax.axis_size(FSDP) * weight.shape[1]
    along_right = jnp.dot(grad_sum, right_next)
    grad_sq_raw, inner_prod, cross_term = packed_total(
        (
            jnp.sum(grad_sum * grad_sum),
            jnp.sum(grad_sum * weight_wide),
            jnp.sum(left_next * along_right),
        ),
        FSDP,
    )
    rank_coeff = inner_prod / (spectral * spectral)
    gradient = grad_sum / spectral - rank_coeff * left_next[:, None] * right_next[None, :]
    left_unit = left_sq / (left_sq + epsilon)
    right_unit = jnp.sum(right_next * right_next)
    grad_sq = (
        grad_sq_raw / (spectral * spectral)
        - 2.0 * rank_coeff * cross_term / spectral
        + rank_coeff * rank_coeff * left_unit * right_unit
    )
    grad_rms = jnp.sqrt(grad_sq / entry_count + epsilon)
    update = (gradient / grad_rms).astype(jnp.bfloat16)
    return (layer_out, input_grad, update, left_next, right_next)


def solution(mesh):
    torus = Mesh(
        mesh.devices.reshape(4, 4, 2, mesh.shape["dp"]), ("fsdp_0", "fsdp_1", "fsdp_2", "dp")
    )
    placed = (P(FSDP_DP, None), P(FSDP_DP, None), P(FSDP, None), P(FSDP))
    return jax.shard_map(
        per_device,
        mesh=torus,
        in_specs=placed,
        out_specs=(P(FSDP_DP, None), P(FSDP_DP, None), P(FSDP, None), P(FSDP), P()),
        check_vma=False,
    )
```

profile of v0, /device:TPU:1, one launch (start us, length us, event | category | flops | bytes accessed | tf_op | source)
XLA Modules:
  0.0 247.7 jit_solution(5602320976544870512)
XLA Ops:
  8.1 0.7 all-gather.6.cloned.1.call-update
  8.8 0.8 copy-done
  9.6 14.6 %convolution_convert_fusion = bf16[4096,2048]{1,0:T(8,128)(2,1)} fusion(bf16[512,4096]{1,0:T(8,128)(2,1)} %param.4, bf16[512,2048]{1,0:T(8,128)(2,1)S(1)} %copy-done), kind=kOutput, calls=%fused_computation | convolution fusion | flops 8598323200 | bytes 23068672 | tf_op jit(solution)/shard_map/dot_general | solution.py:73
  24.3 60.4 %all-gather.6.cloned.1.call-done = bf16[2048,2048]{1,0:T(8,128)(2,1)} async-done(((bf16[128,2048]{1,0:T(8,128)(2,1)}), bf16[2048,2048]{1,0:T(8,128)(2,1)}) %all-gather.6.cloned.1.call-update) | async-done | bytes 8388624 | tf_op jit(solution)/shard_map/all_gather | solution.py:30
  84.7 1.0 copy-done.2
  86.1 17.9 %all_to_all.23 = f32[32,1,2048]{2,1,0:T(1,128)S(1)} all-to-all(f32[32,1,2048]{2,1,0:T(1,128)S(1)} %broadcast_in_dim.18), channel_id=1, replica_groups=mesh['fsdp_0'=4,'fsdp_1'=4,'fsdp_2'=2,'dp'=4] {'fsdp_0','fsdp_1','fsdp_2'}, dimensions={0} | all-to-all | bytes 524288 | tf_op jit(solution)/shard_map/all_to_all | solution.py:14
  106.0 0.8 multiply_reduce_fusion.4
  107.5 10.9 %all_to_all.24 = f32[32,1,1]{2,1,0:T(1,128)S(1)} all-to-all(f32[32,1,1]{2,1,0:T(1,128)S(1)} %broadcast_in_dim.19), channel_id=1, replica_groups=mesh['fsdp_0'=4,'fsdp_1'=4,'fsdp_2'=2,'dp'=4] {'fsdp_0','fsdp_1','fsdp_2'}, dimensions={0} | all-to-all | bytes 256 | tf_op jit(solution)/shard_map/all_to_all | solution.py:14
  118.4 26.0 %reduce-scatter.2.cloned.1.call-done = bf16[128,2048]{1,0:T(8,128)(2,1)} async-done(((bf16[4096,2048]{1,0:T(8,128)(2,1)}), bf16[128,2048]{1,0:T(8,128)(2,1)}) %reduce-scatter.2.cloned.1.call-update) | async-done | bytes 524304 | tf_op jit(solution)/shard_map/reduce_scatter | solution.py:72
  144.4 2.6 %broadcast_in_dim.20 = bf16[4,128,2048]{2,1,0:T(8,128)(2,1)} broadcast(bf16[128,2048]{1,0:T(8,128)(2,1)} %reduce-scatter.2.cloned.1.call-done), dimensions={1,2} | broadcast | bytes 2621440 | tf_op jit(solution)/shard_map/broadcast_in_dim | solution.py:13
  147.0 4.4 %all-to-all-start.2 = ((bf16[4,128,2048]{2,1,0:T(8,128)(2,1)}), bf16[4,128,2048]{2,1,0:T(8,128)(2,1)}, u32[]{:S(2)}, u32[]{:S(2)}) async-start(bf16[4,128,2048]{2,1,0:T(8,128)(2,1)} %broadcast_in_dim.20), calls=%async_computation.3 | async-start | bytes 4194304 | tf_op jit(solution)/shard_map/all_to_all | solution.py:14
  151.5 0.7 reduce_sum.93
  152.8 23.0 %all-to-all-done.2 = bf16[4,128,2048]{2,1,0:T(8,128)(2,1)} async-done(((bf16[4,128,2048]{2,1,0:T(8,128)(2,1)}), bf16[4,128,2048]{2,1,0:T(8,128)(2,1)}, u32[]{:S(2)}, u32[]{:S(2)}) %all-to-all-start.2) | async-done | bytes 2097184 | tf_op jit(solution)/shard_map/all_to_all | solution.py:14
  175.8 2.1 convert_reduce_fusion
  177.9 0.9 fusion.1
  178.8 1.9 multiply_reduce_fusion.1
  180.7 1.9 pad_maximum_fusion
  183.2 8.0 %all-to-all-start.3 = ((f32[32,1,3]{2,1,0:T(1,128)}), f32[32,1,3]{2,1,0:T(1,128)S(1)}, u32[]{:S(2)}, u32[]{:S(2)}) async-start(f32[32,1,3]{2,1,0:T(1,128)} %broadcast_in_dim.21), calls=%async_computation.4 | async-start | bytes 32768 | tf_op jit(solution)/shard_map/all_to_all | solution.py:14
  191.9 6.3 %all-to-all-done.3 = f32[32,1,3]{2,1,0:T(1,128)S(1)} async-done(((f32[32,1,3]{2,1,0:T(1,128)}), f32[32,1,3]{2,1,0:T(1,128)S(1)}, u32[]{:S(2)}, u32[]{:S(2)}) %all-to-all-start.3) | async-done | bytes 416 | tf_op jit(solution)/shard_map/all_to_all | solution.py:14
  201.4 1.0 divide_convert_fusion.2
  202.4 8.3 %copy.16 = bf16[16,2,128,2048]{3,2,1,0:T(8,128)(2,1)S(1)} copy(bf16[16,2,128,2048]{3,2,0,1:T(8,128)(2,1)} %bitcast.45) | data formatting | bytes 33554432 | tf_op jit(solution)/shard_map/transpose | solution.py:34
  210.7 5.7 %copy-done.1 = bf16[16,2,128,2048]{3,2,1,0:T(8,128)(2,1)} copy-done((bf16[16,2,128,2048]{3,2,1,0:T(8,128)(2,1)}, bf16[16,2,128,2048]{3,2,1,0:T(8,128)(2,1)S(1)}, u32[]{:S(2)}) %copy-start.1) | copy-done | bytes 16777240
  216.4 10.1 %divide_convert_fusion.1 = bf16[512,2048]{1,0:T(8,128)(2,1)} fusion(bf16[512,4096]{1,0:T(8,128)(2,1)S(1)} %copy-done.6, bf16[4096,2048]{1,0:T(8,128)(2,1)S(1)} %bitcast.46, f32[]{:T(128)S(6)} %sqrt.10), kind=kOutput, calls=%fused_computation.3 | convolution fusion | flops 8592031744 | bytes 23068676 | tf_op jit(solution)/shard_map/dot_general | solution.py:65
  226.5 13.8 %divide_convert_fusion = bf16[512,4096]{1,0:T(8,128)(2,1)} fusion(bf16[512,2048]{1,0:T(8,128)(2,1)S(1)} %copy-done, bf16[4096,2048]{1,0:T(8,128)(2,1)} %bitcast.47, f32[]{:T(128)S(6)} %sqrt.10), kind=kOutput, calls=%fused_computation.1 | convolution fusion | flops 8594128896 | bytes 23068676 | tf_op jit(solution)/shard_map/dot_general | solution.py:67
  (28 shorter events, 3.8 us)
Async XLA Ops:
  8.0 1.6 copy-start
  8.0 76.7 %all-gather.6.cloned.1.call-start = ((), (), s32[]{:S(2)}) async-start(), calls=%async_computation.7 | async-start | bytes 8912896 | tf_op jit(solution)/shard_map/all_gather | solution.py:30
  8.7 135.7 %reduce-scatter.2.cloned.1.call-start = ((), (), s32[]{:S(2)}) async-start(), calls=%async_computation.6 | async-start | bytes 17301504 | tf_op jit(solution)/shard_map/reduce_scatter | solution.py:72
  24.2 178.2 %all-gather.4.cloned.1.call-start = ((), (), s32[]{:S(2)}) async-start(), calls=%async_computation.5 | async-start | bytes 25165824 | tf_op jit(solution)/shard_map/all_gather | solution.py:30
  84.7 1.0 copy-start.2
  84.7 1.0 copy-start.5
  106.0 95.4 %copy-start.3 = (f32[2048]{0:T(1024)}, f32[2048]{0:T(1024)S(1)}, u32[]{:S(2)}) copy-start(f32[2048]{0:T(1024)S(1)} %get-tuple-element.8) | copy-start | bytes 24580
  147.0 28.8 %all-to-all-start.2 = ((bf16[4,128,2048]{2,1,0:T(8,128)(2,1)}), bf16[4,128,2048]{2,1,0:T(8,128)(2,1)}, u32[]{:S(2)}, u32[]{:S(2)}) async-start(bf16[4,128,2048]{2,1,0:T(8,128)(2,1)} %broadcast_in_dim.20), calls=%async_computation.3 | async-start | bytes 4194304 | tf_op jit(solution)/shard_map/all_to_all | solution.py:14
  152.8 57.9 %copy-start.4 = (f32[128]{0:T(128)}, f32[128]{0:T(128)S(1)}, u32[]{:S(2)}) copy-start(f32[128]{0:T(128)S(1)} %broadcast_divide_fusion.1) | copy-start | bytes 1540
  183.2 14.9 %all-to-all-start.3 = ((f32[32,1,3]{2,1,0:T(1,128)}), f32[32,1,3]{2,1,0:T(1,128)S(1)}, u32[]{:S(2)}, u32[]{:S(2)}) async-start(f32[32,1,3]{2,1,0:T(1,128)} %broadcast_in_dim.21), calls=%async_computation.4 | async-start | bytes 32768 | tf_op jit(solution)/shard_map/all_to_all | solution.py:14
  202.4 14.0 %copy-start.6 = (bf16[512,4096]{1,0:T(8,128)(2,1)S(1)}, bf16[512,4096]{1,0:T(8,128)(2,1)}, u32[]{:S(2)}) copy-start(bf16[512,4096]{1,0:T(8,128)(2,1)} %param.4) | copy-start | bytes 12582916
  210.7 5.7 %copy-start.1 = (bf16[16,2,128,2048]{3,2,1,0:T(8,128)(2,1)}, bf16[16,2,128,2048]{3,2,1,0:T(8,128)(2,1)S(1)}, u32[]{:S(2)}) copy-start(bf16[16,2,128,2048]{3,2,1,0:T(8,128)(2,1)S(1)} %copy.16) | copy-start | bytes 50331652
Sparse Core Ops, SparseCore 0:
  11.0 73.6 all-gather.5
  86.3 33.1 all-gather.3
Sparse Core Ops, SparseCore 1:
  24.3 120.0 reduce-scatter.1
where the time goes:
time: 248 us
  waiting for transfers between devices  116 us (47%)
  matrix products  40.3 us (16%)
  blocking collectives  28.8 us (12%)
  local copies, waits for them, and re-layouts  20.4 us (8%)
  between operations  20.2 us (8%)
  starting transfers between devices  12.6 us (5%)
  other arithmetic  9.01 us (4%)
    all_gather x2, waiting for transfers between devices, gather_in_order(): blocks = lax.all_gather(blocks, axes[k], axis=0, tiled=True)  60.4 us
    all_to_all x2, waiting for transfers between devices, sent_to_all(): return lax.all_to_all(copies, axis, split_axis=0, concat_axis=0, tiled=True)  29.3 us
    all_to_all x2, blocking collectives, sent_to_all(): return lax.all_to_all(copies, axis, split_axis=0, concat_axis=0, tiled=True)  28.8 us
    reduce_scatter x1, waiting for transfers between devices, per_device(): lax.psum_scatter(lax.dot_general(tokens, cotangent, (((0,), (0,)), ((), (...  26 us
    dot_general x1, matrix products, per_device(): lax.dot_general(tokens, cotangent, (((0,), (0,)), ((), ())), preferred_el...  14.6 us
    dot_general x1, matrix products, per_device(): lax.dot_general(cotangent, gathered, (((1,), (1,)), ((), ())), preferred_...  13.8 us
    all_to_all x2, starting transfers between devices, sent_to_all(): return lax.all_to_all(copies, axis, split_axis=0, concat_axis=0, tiled=True)  12.5 us
    dot_general x1, matrix products, per_device(): product = jnp.dot(tokens, gathered, preferred_element_type=jnp.float32)  10.1 us
  transfers between devices with their start and end apart: 5, of which 4 were waited for; matrix products, arithmetic and copies ran while one was open for 12% of the time, Pallas kernels for 0%

commit v1 on v0

--- a/solution.py
+++ b/solution.py
@@ -27,7 +27,11 @@
 def gather_in_order(value, axes, order):
     blocks = value[None]
     for k in order:
-        blocks = lax.all_gather(blocks, axes[k], axis=0, tiled=True)
+        mine = axes[k]
+        ready = jax.lax.axis_size(mine)
+        e_next = jnp.stack([blocks] * ready)
+        moved = jax.lax.all_to_all(e_next, split_axis=0, axis_name=mine, concat_axis=0)
+        blocks = jnp.concatenate(moved, axis=0)
     block = [lax.axis_size(axes[k]) for k in reversed(order)]
     blocks = blocks.reshape(*block, *value.shape)
     turned = sorted(range(len(order)), key=lambda place: order[len(order) - 1 - place])

time: 248 us -> 349 us (1.41)
  waiting for transfers between devices: 116 us -> 163 us
  blocking collectives: 28.8 us -> 47.2 us
  starting transfers between devices: 12.6 us -> 26 us
  other arithmetic: 9.01 us -> 18.8 us
  local copies, waits for them, and re-layouts: 20.4 us -> 28.8 us
  matrix products: 40.3 us -> 45 us
    all_to_all x0 -> x1, waiting for transfers between devices: none -> 148 us  [gather_in_order(): jax.lax.all_to_all(e_next, split_axis=0, axis_name=mine, concat_axis=0)]
    all_gather x2 -> x0, waiting for transfers between devices: 60.4 us -> none  [gather_in_order(): blocks = lax.all_gather(blocks, axes[k], axis=0, tiled=True)]
    reduce_scatter x1, waiting for transfers between devices: 26 us -> 5.87 us  [per_device(): lax.psum_scatter(lax.dot_general(tokens, cotangent, (((0,), (0,)), ((), (...]
    all_to_all x2, waiting for transfers between devices: 29.3 us -> 9.71 us  [sent_to_all(): return lax.all_to_all(copies, axis, split_axis=0, concat_axis=0, tiled=True)]
    all_to_all x0 -> x1, blocking collectives: none -> 19.5 us  [gather_in_order(): jax.lax.all_to_all(e_next, split_axis=0, axis_name=mine, concat_axis=0)]
    another operation x0 -> x1, other arithmetic: none -> 9.73 us  [gather_in_order(): e_next = jnp.stack([blocks] * ready)]
    all_to_all x2, starting transfers between devices: 12.5 us -> 21.2 us  [sent_to_all(): return lax.all_to_all(copies, axis, split_axis=0, concat_axis=0, tiled=True)]
    transpose x1 -> x0, local copies, waits for them, and re-layouts: 8.26 us -> none  [gather_in_order(): blocks.transpose(*turned, *range(len(order), blocks.ndim))]
  transfers between devices with their start and end apart: 5 -> 4, of which waited for: 4 -> 3; matrix products, arithmetic and copies ran while one was open for 12% -> 18% of each run, Pallas kernels for 0% -> 0%
where the time goes in v1:
time: 349 us; the launch traced here: 348 us
  waiting for transfers between devices  163 us (47%)
  blocking collectives  47.2 us (14%)
  matrix products  45 us (13%)
  local copies, waits for them, and re-layouts  28.8 us (8%)
  starting transfers between devices  26 us (7%)
  between operations  18.9 us (5%)
  other arithmetic  18.8 us (5%)
    all_to_all x1, waiting for transfers between devices, gather_in_order(): jax.lax.all_to_all(e_next, split_axis=0, axis_name=mine, concat_axis=0)  148 us
    all_to_all x2, blocking collectives, sent_to_all(): return lax.all_to_all(copies, axis, split_axis=0, concat_axis=0, tiled=True)  27.8 us
    all_to_all x2, starting transfers between devices, sent_to_all(): return lax.all_to_all(copies, axis, split_axis=0, concat_axis=0, tiled=True)  21.2 us
    all_to_all x1, blocking collectives, gather_in_order(): jax.lax.all_to_all(e_next, split_axis=0, axis_name=mine, concat_axis=0)  19.5 us
    dot_general x1, matrix products, per_device(): product = jnp.dot(tokens, gathered, preferred_element_type=jnp.float32)  14.7 us
    dot_general x1, matrix products, per_device(): lax.dot_general(tokens, cotangent, (((0,), (0,)), ((), ())), preferred_el...  14.6 us
    dot_general x1, matrix products, per_device(): lax.dot_general(cotangent, gathered, (((1,), (1,)), ((), ())), preferred_...  13.8 us
    unnamed x12, local copies, waits for them, and re-layouts  12.8 us
  transfers between devices with their start and end apart: 4, of which 3 were waited for; matrix products, arithmetic and copies ran while one was open for 18% of the time, Pallas kernels for 0%

profile of v1, /device:TPU:1, one launch (start us, length us, event | category | flops | bytes accessed | tf_op | source)
XLA Modules:
  0.0 348.0 jit_solution(14830432353792261536)
XLA Ops:
  7.2 1.5 copy-done
  8.8 14.6 %convolution_convert_fusion = bf16[4096,2048]{1,0:T(8,128)(2,1)} fusion(bf16[512,4096]{1,0:T(8,128)(2,1)} %param.4, bf16[512,2048]{1,0:T(8,128)(2,1)S(1)} %copy-done), kind=kOutput, calls=%fused_computation.1 | convolution fusion | flops 8598323200 | bytes 23068672 | tf_op jit(solution)/shard_map/dot_general | solution.py:77
  23.4 1.0 copy-done.1
  24.8 17.3 %all_to_all.33 = f32[32,1,2048]{2,1,0:T(1,128)S(1)} all-to-all(f32[32,1,2048]{2,1,0:T(1,128)S(1)} %broadcast_in_dim.14), channel_id=1, replica_groups=mesh['fsdp_0'=4,'fsdp_1'=4,'fsdp_2'=2,'dp'=4] {'fsdp_0','fsdp_1','fsdp_2'}, dimensions={0} | all-to-all | bytes 524288 | tf_op jit(solution)/shard_map/all_to_all | solution.py:14
  45.8 10.4 %all_to_all.34 = f32[32,1,1]{2,1,0:T(1,128)S(1)} all-to-all(f32[32,1,1]{2,1,0:T(1,128)S(1)} %broadcast_in_dim.15), channel_id=1, replica_groups=mesh['fsdp_0'=4,'fsdp_1'=4,'fsdp_2'=2,'dp'=4] {'fsdp_0','fsdp_1','fsdp_2'}, dimensions={0} | all-to-all | bytes 256 | tf_op jit(solution)/shard_map/all_to_all | solution.py:14
  56.2 4.8 %stack.6 = bf16[16,1,128,2048]{3,2,1,0:T(8,128)(2,1)} broadcast(bf16[128,2048]{1,0:T(8,128)(2,1)S(1)} %copy-done.1), dimensions={2,3} | broadcast | bytes 8912896 | tf_op jit(solution)/shard_map/stack | solution.py:32
  61.0 4.8 %all-to-all-start = ((bf16[16,1,128,2048]{3,2,1,0:T(8,128)(2,1)}), bf16[16,1,128,2048]{3,2,1,0:T(8,128)(2,1)}, u32[]{:S(2)}, u32[]{:S(2)}) async-start(bf16[16,1,128,2048]{3,2,1,0:T(8,128)(2,1)} %stack.6), calls=%async_computation | async-start | bytes 16777216 | tf_op jit(solution)/shard_map/all_to_all | solution.py:33
  67.8 147.6 %all-to-all-done = bf16[16,1,128,2048]{3,2,1,0:T(8,128)(2,1)} async-done(((bf16[16,1,128,2048]{3,2,1,0:T(8,128)(2,1)}), bf16[16,1,128,2048]{3,2,1,0:T(8,128)(2,1)}, u32[]{:S(2)}, u32[]{:S(2)}) %all-to-all-start) | async-done | bytes 8388640 | tf_op jit(solution)/shard_map/all_to_all | solution.py:33
  215.4 9.7 %pad_maximum_fusion = bf16[2,16,128,2048]{3,2,1,0:T(8,128)(2,1)S(1)} fusion(bf16[1,16,128,2048]{3,2,1,0:T(8,128)(2,1)} %bitcast), kind=kLoop, calls=%fused_computation | loop fusion | flops 8388608 | bytes 25165824 | tf_op jit(solution)/shard_map/stack | solution.py:32
  225.1 19.5 %all_to_all.35 = bf16[2,16,128,2048]{3,2,1,0:T(8,128)(2,1)S(1)} all-to-all(bf16[2,16,128,2048]{3,2,1,0:T(8,128)(2,1)S(1)} %pad_maximum_fusion), channel_id=1, replica_groups=mesh['fsdp_0'=4,'fsdp_1'=4,'fsdp_2'=2,'dp'=4] {'fsdp_2'}, dimensions={0} | all-to-all | bytes 33554432 | tf_op jit(solution)/shard_map/all_to_all | solution.py:33
  244.6 6.6 %copy.25 = bf16[2,16,128,2048]{3,2,0,1:T(8,128)(2,1)} copy(bf16[2,16,128,2048]{3,2,1,0:T(8,128)(2,1)S(1)} %all_to_all.35) | data formatting | bytes 33554432 | tf_op jit(solution)/shard_map/all_to_all | solution.py:33
  251.2 5.9 %reduce-scatter.2.cloned.1.call-done = bf16[128,2048]{1,0:T(8,128)(2,1)} async-done(((bf16[4096,2048]{1,0:T(8,128)(2,1)}), bf16[128,2048]{1,0:T(8,128)(2,1)}) %reduce-scatter.2.cloned.1.call-update) | async-done | bytes 524304 | tf_op jit(solution)/shard_map/reduce_scatter | solution.py:76
  257.1 2.6 broadcast_in_dim.16
  259.7 4.6 %all-to-all-start.4 = ((bf16[4,128,2048]{2,1,0:T(8,128)(2,1)}), bf16[4,128,2048]{2,1,0:T(8,128)(2,1)}, u32[]{:S(2)}, u32[]{:S(2)}) async-start(bf16[4,128,2048]{2,1,0:T(8,128)(2,1)} %broadcast_in_dim.16), calls=%async_computation.5 | async-start | bytes 4194304 | tf_op jit(solution)/shard_map/all_to_all | solution.py:14
  264.3 14.7 %fusion.1 = bf16[512,2048]{0,1:T(8,128)(2,1)} fusion(bf16[4096,2048]{1,0:T(8,128)(2,1)} %bitcast.48, bf16[512,4096]{1,0:T(8,128)(2,1)} %param.4, f32[]{:T(128)S(6)} %sqrt.10), kind=kOutput, calls=%fused_computation.6 | convolution fusion | flops 8592031744 | bytes 23068676 | tf_op jit(solution)/shard_map/dot_general | solution.py:69
  279.0 9.7 %all-to-all-done.4 = bf16[4,128,2048]{2,1,0:T(8,128)(2,1)} async-done(((bf16[4,128,2048]{2,1,0:T(8,128)(2,1)}), bf16[4,128,2048]{2,1,0:T(8,128)(2,1)}, u32[]{:S(2)}, u32[]{:S(2)}) %all-to-all-start.4) | async-done | bytes 2097184 | tf_op jit(solution)/shard_map/all_to_all | solution.py:14
  288.7 2.1 convert_reduce_fusion
  290.8 1.9 multiply_reduce_fusion.1
  293.5 1.9 pad_maximum_fusion.1
  296.1 16.6 %all-to-all-start.5 = ((f32[32,1,3]{2,1,0:T(1,128)}), f32[32,1,3]{2,1,0:T(1,128)S(1)}, u32[]{:S(2)}, u32[]{:S(2)}) async-start(f32[32,1,3]{2,1,0:T(1,128)} %broadcast_in_dim.17), calls=%async_computation.6 | async-start | bytes 32768 | tf_op jit(solution)/shard_map/all_to_all | solution.py:14
  312.7 13.8 %fusion = bf16[512,4096]{0,1:T(8,128)(2,1)} fusion(bf16[4096,2048]{1,0:T(8,128)(2,1)} %bitcast.49, bf16[512,2048]{1,0:T(8,128)(2,1)S(1)} %copy-done, f32[]{:T(128)S(6)} %sqrt.10), kind=kOutput, calls=%fused_computation.3 | convolution fusion | flops 8594128896 | bytes 23068676 | tf_op jit(solution)/shard_map/dot_general | solution.py:71
  326.5 3.9 %copy.29 = bf16[512,2048]{1,0:T(8,128)(2,1)} copy(bf16[512,2048]{0,1:T(8,128)(2,1)} %fusion.1) | data formatting | bytes 4194304
  330.4 6.3 %copy.30 = bf16[512,4096]{1,0:T(8,128)(2,1)} copy(bf16[512,4096]{0,1:T(8,128)(2,1)} %fusion) | data formatting | bytes 8388608
  340.1 1.0 divide_convert_fusion.2
  (25 shorter events, 6.1 us)
Async XLA Ops:
  7.2 1.6 copy-start
  7.2 249.9 %reduce-scatter.2.cloned.1.call-start = ((), (), s32[]{:S(2)}) async-start(), calls=%async_computation.7 | async-start | bytes 17301504 | tf_op jit(solution)/shard_map/reduce_scatter | solution.py:76
  23.4 1.0 copy-start.1
  23.4 1.0 copy-start.4
  44.2 295.9 %copy-start.2 = (f32[2048]{0:T(1024)}, f32[2048]{0:T(1024)S(1)}, u32[]{:S(2)}) copy-start(f32[2048]{0:T(1024)S(1)} %get-tuple-element.38) | copy-start | bytes 24580
  61.0 154.4 %all-to-all-start = ((bf16[16,1,128,2048]{3,2,1,0:T(8,128)(2,1)}), bf16[16,1,128,2048]{3,2,1,0:T(8,128)(2,1)}, u32[]{:S(2)}, u32[]{:S(2)}) async-start(bf16[16,1,128,2048]{3,2,1,0:T(8,128)(2,1)} %stack.6), calls=%async_computation | async-start | bytes 16777216 | tf_op jit(solution)/shard_map/all_to_all | solution.py:33
  67.8 224.9 %copy-start.3 = (f32[128]{0:T(128)}, f32[128]{0:T(128)S(1)}, u32[]{:S(2)}) copy-start(f32[128]{0:T(128)S(1)} %broadcast_divide_fusion.1) | copy-start | bytes 1540
  259.7 29.0 %all-to-all-start.4 = ((bf16[4,128,2048]{2,1,0:T(8,128)(2,1)}), bf16[4,128,2048]{2,1,0:T(8,128)(2,1)}, u32[]{:S(2)}, u32[]{:S(2)}) async-start(bf16[4,128,2048]{2,1,0:T(8,128)(2,1)} %broadcast_in_dim.16), calls=%async_computation.5 | async-start | bytes 4194304 | tf_op jit(solution)/shard_map/all_to_all | solution.py:14
  296.1 40.7 %all-to-all-start.5 = ((f32[32,1,3]{2,1,0:T(1,128)}), f32[32,1,3]{2,1,0:T(1,128)S(1)}, u32[]{:S(2)}, u32[]{:S(2)}) async-start(f32[32,1,3]{2,1,0:T(1,128)} %broadcast_in_dim.17), calls=%async_computation.6 | async-start | bytes 32768 | tf_op jit(solution)/shard_map/all_to_all | solution.py:14
Sparse Core Ops, SparseCore 0:
  23.5 233.4 reduce-scatter.1
